TPU v7x, 32 devices: a whole 2x2x4 slice. The times are simulated.
32 devices in a mesh: zero: 8 (over y, x, core), width: 4 (over z).
Axes of the slice: x: 2, y: 2, z: 4, core: 2. Of those that a mesh axis runs over, the one named last changes fastest.
Arguments:
- train_query: bfloat16 [4608, 4096], P('zero', 'width'), may hold values from -0.09375 to 0.09375
- low_query: bfloat16 [4608, 64], P('zero'), may hold values from -0.09375 to 0.09375
- high_query: bfloat16 [64, 4096], P(None, 'width'), may hold values from -0.75 to 0.75
- train_key: bfloat16 [4608, 2048], P('zero', 'width'), may hold values from -0.09375 to 0.09375
- low_key: bfloat16 [4608, 64], P('zero'), may hold values from -0.09375 to 0.09375
- high_key: bfloat16 [64, 2048], P(None, 'width'), may hold values from -0.75 to 0.75
- train_value: bfloat16 [4608, 2048], P('zero', 'width'), may hold values from -0.09375 to 0.09375
- low_value: bfloat16 [4608, 64], P('zero'), may hold values from -0.09375 to 0.09375
- high_value: bfloat16 [64, 2048], P(None, 'width'), may hold values from -0.75 to 0.75
- train_mixed: bfloat16 [4096, 4608], P('width', 'zero'), may hold values from -0.09375 to 0.09375
- low_mixed: bfloat16 [4096, 64], P('width'), may hold values from -0.09375 to 0.09375
- high_mixed: bfloat16 [64, 4608], P(None, 'zero'), may hold values from -0.75 to 0.75
- norm_train: float32 [4608], P(('zero', 'width')), may hold values from 0.25 to 1.75
- norm_step: float32 [4608], P(('zero', 'width')), may hold values from -0.3 to 0.3
Outputs:
- final_query: bfloat16 [4608, 4096], P(None, 'width')
- final_key: bfloat16 [4608, 2048], P(None, 'width')
- final_value: bfloat16 [4608, 2048], P(None, 'width')
- final_mixed: bfloat16 [4096, 4608], P('width')
- serve_norm: bfloat16 [4608], replicated
All inputs are finite; a program needn't handle non-finite values.
Results may differ from a plain program's by a relative error of at most 0.001.
Values may be sent and summed in bfloat16 or wider, within the bound.
A program may use at most 192 MiB of HBM per device.

v0:
```python
import jax
import jax.numpy as jnp
from jax import lax
from jax.sharding import PartitionSpec as P

mix_rate = 0.5


def on_device(
    train_query,
    low_query,
    high_query,
    train_key,
    low_key,
    high_key,
    train_value,
    low_value,
    high_value,
    train_mixed,
    low_mixed,
    high_mixed,
    norm_train,
    norm_step,
):
    (
        moved_query,
        moved_key,
        moved_value,
        moved_mixed,
        factor_query,
        factor_key,
        factor_value,
        factor_mixed,
    ) = (
        lax.all_gather(train_query, "zero", axis=0, tiled=True),
        lax.all_gather(train_key, "zero", axis=0, tiled=True),
        lax.all_gather(train_value, "zero", axis=0, tiled=True),
        lax.all_gather(train_mixed, "zero", axis=1, tiled=True),
        lax.all_gather(low_query, "zero", axis=0, tiled=True),
        lax.all_gather(low_key, "zero", axis=0, tiled=True),
        lax.all_gather(low_value, "zero", axis=0, tiled=True),
        lax.all_gather(high_mixed, "zero", axis=1, tiled=True),
    )
    result_query = moved_query.astype(jnp.float32) + mix_rate * jnp.dot(
        factor_query, high_query, preferred_element_type=jnp.float32
    )
    final_query = result_query.astype(jnp.bfloat16)
    result_key = moved_key.astype(jnp.float32) + mix_rate * jnp.dot(
        factor_key, high_key, preferred_element_type=jnp.float32
    )
    final_key = result_key.astype(jnp.bfloat16)
    result_value = moved_value.astype(jnp.float32) + mix_rate * jnp.dot(
        factor_value, high_value, preferred_element_type=jnp.float32
    )
    final_value = result_value.astype(jnp.bfloat16)
    result_mixed = moved_mixed.astype(jnp.float32) + mix_rate * jnp.dot(
        low_mixed, factor_mixed, preferred_element_type=jnp.float32
    )
    final_mixed = result_mixed.astype(jnp.bfloat16)
    serve_norm = lax.all_gather(
        (norm_train + norm_step).astype(jnp.bfloat16), ("zero", "width"), axis=0, tiled=True
    )
    return (final_query, final_key, final_value, final_mixed, serve_norm)


def solution(mesh):
    return jax.shard_map(
        on_device,
        mesh=mesh,
        in_specs=(
            P("zero", "width"),
            P("zero", None),
            P(None, "width"),
            P("zero", "width"),
            P("zero", None),
            P(None, "width"),
            P("zero", "width"),
            P("zero", None),
            P(None, "width"),
            P("width", "zero"),
            P("width", None),
            P(None, "zero"),
            P(("zero", "width")),
            P(("zero", "width")),
        ),
        out_specs=(P(None, "width"), P(None, "width"), P(None, "width"), P("width", None), P()),
        check_vma=False,
    )
```

profile of v0, /device:TPU:0, one launch (start us, length us, event | category | flops | bytes accessed | tf_op | source)
XLA Modules:
  0.0 232.1 jit_solution(15176679643474011088)
XLA Ops:
  7.3 0.7 all-gather.13.cloned.1.call-update
  8.0 0.7 all-gather.11.cloned.1.call-update
  8.8 0.7 all-gather.15.cloned.1.call-update
  9.5 0.5 all-gather.9.cloned.1.call-update
  10.0 12.0 %all-gather.3 = bf16[8,576,64]{1,2,0:T(8,128)(2,1)S(1)} all-gather(bf16[1,576,64]{1,2,0:T(8,128)(2,1)} %bitcast.22), channel_id=1, replica_groups=mesh['zero'=8,'width'=4] {'zero'}, dimensions={0}, use_global_device_ids=true | all-gather | bytes 663552 | tf_op jit(solution)/shard_map/all_gather | solution.py:42
  22.0 0.4 copy.29
  22.4 0.4 reshape.19
  22.8 10.9 %all-gather = bf16[8,576,64]{1,2,0:T(8,128)(2,1)S(1)} all-gather(bf16[1,576,64]{1,2,0:T(8,128)(2,1)} %bitcast.23), channel_id=1, replica_groups=mesh['zero'=8,'width'=4] {'zero'}, dimensions={0}, use_global_device_ids=true | all-gather | bytes 663552 | tf_op jit(solution)/shard_map/all_gather | solution.py:39
  33.7 0.4 copy.25
  34.1 0.4 reshape.13
  34.5 13.3 %all-gather.2 = bf16[8,576,64]{1,2,0:T(8,128)(2,1)S(1)} all-gather(bf16[1,576,64]{1,2,0:T(8,128)(2,1)S(1)} %bitcast.24), channel_id=1, replica_groups=mesh['zero'=8,'width'=4] {'zero'}, dimensions={0}, use_global_device_ids=true | all-gather | bytes 663552 | tf_op jit(solution)/shard_map/all_gather | solution.py:41
  47.8 0.4 copy.27
  48.2 0.4 reshape.17
  48.6 10.3 %all-gather.1 = bf16[8,576,64]{1,2,0:T(8,128)(2,1)S(1)} all-gather(bf16[1,576,64]{1,2,0:T(8,128)(2,1)S(1)} %bitcast.25), channel_id=1, replica_groups=mesh['zero'=8,'width'=4] {'zero'}, dimensions={0}, use_global_device_ids=true | all-gather | bytes 663552 | tf_op jit(solution)/shard_map/all_gather | solution.py:40
  58.9 0.4 copy.26
  59.3 0.4 reshape.15
  60.0 40.2 %all-reduce = bf16[4608]{0:T(1024)(128)(2,1)} all-reduce(bf16[4608]{0:T(1024)(128)(2,1)S(1)} %dynamic-update-slice), channel_id=1, replica_groups=mesh['zero'=8,'width'=4] {'zero','width'}, use_global_device_ids=true, to_apply=%add | all-reduce | flops 4608 | bytes 18432
  100.2 5.9 %add_convert_fusion.2 = bf16[4608,512]{1,0:T(8,128)(2,1)} fusion(bf16[4608,512]{1,0:T(8,128)(2,1)} %all-gather.13.cloned.1.call-done, bf16[4608,64]{0,1:T(8,128)(2,1)S(1)} %reshape.17, bf16[64,512]{1,0:T(8,128)(2,1)S(1)} %copy-done.4), kind=kOutput, calls=%fused_computation.2 | convolution fusion | flops 311427072 | bytes 10092544 | tf_op jit(solution)/shard_map/dot_general | solution.py:52
  106.2 6.4 %add_convert_fusion.3 = bf16[4608,512]{1,0:T(8,128)(2,1)} fusion(bf16[4608,512]{1,0:T(8,128)(2,1)} %all-gather.11.cloned.1.call-done, bf16[4608,64]{0,1:T(8,128)(2,1)S(1)} %reshape.15, bf16[64,512]{1,0:T(8,128)(2,1)S(1)} %copy-done.5), kind=kOutput, calls=%fused_computation.3 | convolution fusion | flops 311427072 | bytes 10092544 | tf_op jit(solution)/shard_map/dot_general | solution.py:48
  112.6 45.0 %all-gather.15.cloned.1.call-done = bf16[1024,4608]{0,1:T(8,128)(2,1)} async-done(((bf16[1024,576]{0,1:T(8,128)(2,1)}), bf16[1024,4608]{0,1:T(8,128)(2,1)}) %all-gather.15.cloned.1.call-update) | async-done | bytes 9437200 | tf_op jit(solution)/shard_map/all_gather | solution.py:38
  157.6 12.7 %copy.28 = bf16[1024,4608]{1,0:T(8,128)(2,1)} copy(bf16[1024,4608]{0,1:T(8,128)(2,1)} %all-gather.15.cloned.1.call-done) | data formatting | bytes 18874368 | tf_op jit(solution)/shard_map/all_gather | solution.py:38
  170.3 7.5 %add_convert_fusion = bf16[1024,4608]{1,0:T(8,128)(2,1)} fusion(bf16[1024,4608]{1,0:T(8,128)(2,1)} %copy.28, bf16[1024,64]{0,1:T(8,128)(2,1)S(1)} %copy-done, bf16[4608,64]{0,1:T(8,128)(2,1)S(1)} %reshape.19), kind=kOutput, calls=%fused_computation | convolution fusion | flops 622854144 | bytes 19595264 | tf_op jit(solution)/shard_map/dot_general | solution.py:56
  177.8 40.2 %all-gather.9.cloned.1.call-done = bf16[4608,1024]{1,0:T(8,128)(2,1)} async-done(((bf16[576,1024]{1,0:T(8,128)(2,1)}), bf16[4608,1024]{1,0:T(8,128)(2,1)}) %all-gather.9.cloned.1.call-update) | async-done | bytes 9437200 | tf_op jit(solution)/shard_map/all_gather | solution.py:35
  218.1 7.5 %add_convert_fusion.1 = bf16[4608,1024]{1,0:T(8,128)(2,1)} fusion(bf16[4608,1024]{1,0:T(8,128)(2,1)} %all-gather.9.cloned.1.call-done, bf16[4608,64]{0,1:T(8,128)(2,1)S(1)} %reshape.13, bf16[64,1024]{1,0:T(8,128)(2,1)S(1)} %copy-done.1), kind=kOutput, calls=%fused_computation.1 | convolution fusion | flops 622854144 | bytes 19595264 | tf_op jit(solution)/shard_map/dot_general | solution.py:44
  (25 shorter events, 0.5 us)
Async XLA Ops:
  7.2 163.1 %copy-start = (bf16[1024,64]{0,1:T(8,128)(2,1)S(1)}, bf16[1024,64]{0,1:T(8,128)(2,1)}, u32[]{:S(2)}) copy-start(bf16[1024,64]{0,1:T(8,128)(2,1)} %param.24) | copy-start | bytes 393220
  7.2 27.4 %copy-start.2 = (bf16[576,64]{0,1:T(8,128)(2,1)S(1)}, bf16[576,64]{0,1:T(8,128)(2,1)}, u32[]{:S(2)}) copy-start(bf16[576,64]{0,1:T(8,128)(2,1)} %param.21) | copy-start | bytes 221188
  7.2 41.4 %copy-start.3 = (bf16[576,64]{0,1:T(8,128)(2,1)S(1)}, bf16[576,64]{0,1:T(8,128)(2,1)}, u32[]{:S(2)}) copy-start(bf16[576,64]{0,1:T(8,128)(2,1)} %param.18) | copy-start | bytes 221188
  7.2 52.5 %copy-start.6 = (f32[144]{0:T(256)S(1)}, f32[144]{0:T(256)}, u32[]{:S(2)}) copy-start(f32[144]{0:T(256)} %param.26) | copy-start | bytes 1732
  7.2 52.5 %copy-start.7 = (f32[144]{0:T(256)S(1)}, f32[144]{0:T(256)}, u32[]{:S(2)}) copy-start(f32[144]{0:T(256)} %param.27) | copy-start | bytes 1732
  7.2 93.0 %copy-start.4 = (bf16[64,512]{1,0:T(8,128)(2,1)S(1)}, bf16[64,512]{1,0:T(8,128)(2,1)}, u32[]{:S(2)}) copy-start(bf16[64,512]{1,0:T(8,128)(2,1)} %param.22) | copy-start | bytes 196612
  7.2 93.0 %all-gather.13.cloned.1.call-start = ((), (), s32[]{:S(2)}) async-start(), calls=%async_computation.2 | async-start | bytes 5308416 | tf_op jit(solution)/shard_map/all_gather | solution.py:37
  8.0 98.2 %all-gather.11.cloned.1.call-start = ((), (), s32[]{:S(2)}) async-start(), calls=%async_computation.1 | async-start | bytes 5308416 | tf_op jit(solution)/shard_map/all_gather | solution.py:36
  8.7 148.9 %all-gather.15.cloned.1.call-start = ((), (), s32[]{:S(2)}) async-start(), calls=%async_computation.3 | async-start | bytes 10616832 | tf_op jit(solution)/shard_map/all_gather | solution.py:38
  9.5 208.6 %all-gather.9.cloned.1.call-start = ((), (), s32[]{:S(2)}) async-start(), calls=%async_computation | async-start | bytes 10616832 | tf_op jit(solution)/shard_map/all_gather | solution.py:35
  33.7 72.4 %copy-start.5 = (bf16[64,512]{1,0:T(8,128)(2,1)S(1)}, bf16[64,512]{1,0:T(8,128)(2,1)}, u32[]{:S(2)}) copy-start(bf16[64,512]{1,0:T(8,128)(2,1)} %param.19) | copy-start | bytes 196612
  170.3 47.8 %copy-start.1 = (bf16[64,1024]{1,0:T(8,128)(2,1)S(1)}, bf16[64,1024]{1,0:T(8,128)(2,1)}, u32[]{:S(2)}) copy-start(bf16[64,1024]{1,0:T(8,128)(2,1)} %param.16) | copy-start | bytes 393220
Sparse Core Ops, SparseCore 0:
  9.9 45.4 all-gather.12
  57.3 39.6 all-gather.10
  98.9 58.6 all-gather.14
  159.3 58.6 all-gather.8
where the time goes:
time: 233 us; the launch traced here: 232 us
  waiting for transfers between devices  87.8 us (38%)
  blocking collectives  86.6 us (37%)
  matrix products  27.4 us (12%)
  local copies, waits for them, and re-layouts  16.2 us (7%)
  between operations  13.9 us (6%)
    all_gather x1, waiting for transfers between devices, on_device(): lax.all_gather(train_mixed, 'zero', axis=1, tiled=True)  45 us
    all_gather x1, waiting for transfers between devices, on_device(): lax.all_gather(train_query, 'zero', axis=0, tiled=True)  40.2 us
    unnamed x1, blocking collectives  40.2 us
    all_gather x1, blocking collectives, on_device(): lax.all_gather(low_value, 'zero', axis=0, tiled=True)  13.3 us
    all_gather x1, local copies, waits for them, and re-layouts, on_device(): lax.all_gather(train_mixed, 'zero', axis=1, tiled=True)  12.7 us
    all_gather x1, blocking collectives, on_device(): lax.all_gather(high_mixed, 'zero', axis=1, tiled=True)  12 us
    all_gather x1, blocking collectives, on_device(): lax.all_gather(low_query, 'zero', axis=0, tiled=True)  10.9 us
    all_gather x1, blocking collectives, on_device(): lax.all_gather(low_key, 'zero', axis=0, tiled=True)  10.3 us
  transfers between devices with their start and end apart: 4, of which 2 were waited for; matrix products, arithmetic and copies ran while one was open for 16% of the time, Pallas kernels for 0%

commit v1 on v0

v1 whole, which is shorter than its diff:
```python
import functools
import math

import jax
import jax.numpy as jnp
from jax import lax
from jax.experimental import pallas as pl
from jax.experimental.pallas import tpu as pltpu
from jax.sharding import PartitionSpec as P

mix_rate = 0.5
MESH = pl.DeviceIdType.MESH


def gather_kernel(n, width, *refs):
    trains, lows, highs, norm = refs[0:4], refs[4:8], refs[8:12], refs[12]
    outs, norm_out = refs[13:17], refs[17]
    mine, norm_row = refs[18:22], refs[22]
    send_sem, recv_sem, norm_send, norm_recv, local_sem = refs[23:28]

    chips = n // 2
    side = math.isqrt(chips)
    if side * side != chips:
        side = chips
    rows = trains[0].shape[0]
    half = rows // 2

    me = lax.axis_index("zero")
    me_width = lax.axis_index("width")
    chip, core = me // 2, me % 2

    def turned(place):
        y, x = place // side, place % side
        return y * side + x + (y % 2) * (side - 1 - 2 * x)

    ring = turned(chip)

    def at(step):
        return turned((ring + step + chips) % chips) * 2 + core

    after, before = at(1), at(-1)
    partner = chip * 2 + (1 - core)

    barrier = pltpu.get_barrier_semaphore()
    for step in range(1, n):
        pl.semaphore_signal(
            barrier, inc=1, device_id={"zero": (me + step) % n}, device_id_type=MESH
        )
    for step in range(1, width):
        pl.semaphore_signal(
            barrier, inc=1, device_id={"width": (me_width + step) % width}, device_id_type=MESH
        )

    started = []
    locals_ = []
    count = [0]

    def block(array, owner, part):
        return outs[array].at[pl.ds(pl.multiple_of(owner * rows + part * half, 8), half)]

    def send(source, target, device):
        slot = count[0]
        count[0] += 1
        copy = pltpu.make_async_remote_copy(
            src_ref=source,
            dst_ref=target,
            send_sem=send_sem.at[slot],
            recv_sem=recv_sem.at[slot],
            device_id={"zero": device},
            device_id_type=MESH,
        )
        copy.start()
        started.append(copy)
        return copy

    def own(array, part):
        return mine[array].at[pl.ds(part * half, half)]

    def compute(array):
        delta = lax.dot_general(
            lows[array][...],
            highs[array][...],
            (((0,), (0,)), ((), ())),
            preferred_element_type=jnp.float32,
        )
        merged = trains[array][...].astype(jnp.float32) + mix_rate * delta
        mine[array][...] = merged.astype(jnp.bfloat16)

    streams = ([], [])
    aways = (after, before)
    partner_copies = []
    hops = chips // 2

    def send_own(direction, array, part):
        copy = send(own(array, part), block(array, me, part), aways[direction])
        streams[direction].append((copy, array, part))

    for array in range(4):
        compute(array)
        if array == 0:
            pl.semaphore_wait(barrier, n - 1 + width - 1)
        send_own(0, array, 0)
        send_own(1, array, 1)
    if hops > 1:
        for array in range(4):
            send_own(0, array, 1)
            send_own(1, array, 0)

    own_row = pltpu.make_async_copy(norm, norm_row.at[me_width], local_sem.at[4])
    own_row.start()
    row_copies = []
    for step in range(1, width):
        copy = pltpu.make_async_remote_copy(
            src_ref=norm,
            dst_ref=norm_row.at[me_width],
            send_sem=norm_send.at[step - 1],
            recv_sem=norm_recv.at[step - 1],
            device_id={"width": (me_width + step) % width},
            device_id_type=MESH,
        )
        copy.start()
        row_copies.append(copy)

    for array in range(4):
        copy = pltpu.make_async_copy(
            mine[array],
            outs[array].at[pl.ds(pl.multiple_of(me * rows, 8), rows)],
            local_sem.at[array],
        )
        copy.start()
        locals_.append(copy)
        for part in range(2):
            partner_copies.append(send(own(array, part), block(array, me, part), partner))

    own_row.wait()
    for copy in row_copies:
        copy.wait()
    own_table = pltpu.make_async_copy(norm_row, norm_out.at[me], local_sem.at[4])
    own_table.start()
    table_copies = []
    for step in range(1, n):
        copy = pltpu.make_async_remote_copy(
            src_ref=norm_row,
            dst_ref=norm_out.at[me],
            send_sem=norm_send.at[width - 2 + step],
            recv_sem=norm_recv.at[width - 2 + step],
            device_id={"zero": (me + step) % n},
            device_id_type=MESH,
        )
        copy.start()
        table_copies.append(copy)

    for hop in range(1, hops + 1):
        arriving = streams
        streams = ([], [])
        for turn in range(len(arriving[0])):
            for direction in range(2):
                copy, array, part = arriving[direction][turn]
                owner = at(-hop if direction == 0 else hop)
                copy.wait_recv()
                here = block(array, owner, part)
                last = hop + 1 == hops
                if hop < hops and (not last or part == direction):
                    further = send(here, here, aways[direction])
                    streams[direction].append((further, array, part))
                partner_copies.append(send(here, here, partner))

    for copy in partner_copies:
        copy.wait_recv()
    for copy in started:
        copy.wait_send()
    for copy in table_copies:
        copy.wait()
    own_table.wait()
    for copy in locals_:
        copy.wait()


def gather(n, width, trains, lows, highs, norm):
    chips = n // 2
    hops = chips // 2
    ring_blocks = 2 * (8 * (hops - 1) + 4)
    slots = ring_blocks + 8 + ring_blocks
    vmem = pl.BlockSpec(memory_space=pltpu.VMEM)
    anywhere = pl.BlockSpec(memory_space=pl.ANY)
    return pl.pallas_call(
        functools.partial(gather_kernel, n, width),
        out_shape=[
            jax.ShapeDtypeStruct((n * train.shape[0], train.shape[1]), jnp.bfloat16)
            for train in trains
        ]
        + [jax.ShapeDtypeStruct((n, width) + norm.shape, norm.dtype)],
        in_specs=[vmem] * 13,
        out_specs=[anywhere] * 5,
        scratch_shapes=[pltpu.VMEM(train.shape, jnp.bfloat16) for train in trains]
        + [
            pltpu.VMEM((width,) + norm.shape, norm.dtype),
            pltpu.SemaphoreType.DMA((slots,)),
            pltpu.SemaphoreType.DMA((slots,)),
            pltpu.SemaphoreType.DMA((n + width - 2,)),
            pltpu.SemaphoreType.DMA((n + width - 2,)),
            pltpu.SemaphoreType.DMA((5,)),
        ],
        compiler_params=pltpu.CompilerParams(collective_id=0, has_side_effects=True),
    )(*trains, *lows, *highs, norm)


def on_device(
    n,
    width,
    train_query,
    low_query,
    high_query,
    train_key,
    low_key,
    high_key,
    train_value,
    low_value,
    high_value,
    train_mixed,
    low_mixed,
    high_mixed,
    norm_train,
    norm_step,
):
    share = norm_train.shape[0]
    lanes = -(-share // 1024) * 1024
    norm = jnp.pad(norm_train + norm_step, (0, lanes - share)).reshape(-1, 128)
    query, key, value, mixed, table = gather(
        n,
        width,
        (train_query, train_key, train_value, train_mixed.T),
        (low_query.T, low_key.T, low_value.T, high_mixed),
        (high_query, high_key, high_value, low_mixed.T),
        norm,
    )
    serve_norm = table.reshape(n * width, -1)[:, :share].reshape(-1).astype(jnp.bfloat16)
    return (query, key, value, mixed.T, serve_norm)


def solution(mesh):
    return jax.shard_map(
        functools.partial(on_device, mesh.shape["zero"], mesh.shape["width"]),
        mesh=mesh,
        in_specs=(
            P("zero", "width"),
            P("zero", None),
            P(None, "width"),
            P("zero", "width"),
            P("zero", None),
            P(None, "width"),
            P("zero", "width"),
            P("zero", None),
            P(None, "width"),
            P("width", "zero"),
            P("width", None),
            P(None, "zero"),
            P(("zero", "width")),
            P(("zero", "width")),
        ),
        out_specs=(P(None, "width"), P(None, "width"), P(None, "width"), P("width", None), P()),
        check_vma=False,
    )
```

time: 233 us -> 161 us (0.69)
  Pallas kernels: 0 us -> 129 us
  waiting for transfers between devices: 87.8 us -> 0 us
  blocking collectives: 86.6 us -> 0 us
  matrix products: 27.4 us -> 0 us
  local copies, waits for them, and re-layouts: 16.2 us -> 29.6 us
  between operations: 13.9 us -> 0.66 us
    pallas_call x0 -> x1, Pallas kernels: none -> 129 us  [gather(): pl.pallas_call(functools.partial(gather_kernel, n, width), out_shape=[jax...]
    all_gather x4 -> x0, waiting for transfers between devices: 85.2 us -> none  [the longest x1 45 us: on_device(): lax.all_gather(train_mixed, 'zero', axis=1, tiled=True)]
    all_gather x4 -> x0, blocking collectives: 46.4 us -> none  [the longest x1 13.3 us: on_device(): lax.all_gather(low_value, 'zero', axis=0, tiled=True)]
    unnamed x1 -> x0, blocking collectives: 40.2 us -> none
    dot_general x4 -> x0, matrix products: 27.4 us -> none  [the longest x1 7.54 us: on_device(): jnp.dot(low_mixed, factor_mixed, preferred_element_type=jnp.float32)]
    unnamed x22 -> x7, local copies, waits for them, and re-layouts: 2 us -> 28.3 us
    all_gather x5 -> x0, local copies, waits for them, and re-layouts: 14.2 us -> none  [the longest x1 12.7 us: on_device(): lax.all_gather(train_mixed, 'zero', axis=1, tiled=True)]
    unnamed x4 -> x0, waiting for transfers between devices: 2.58 us -> none
  transfers between devices with their start and end apart: 4 -> 0, of which waited for: 2 -> 0; matrix products, arithmetic and copies ran while one was open for 16% -> 0% of each run, Pallas kernels for 0% -> 0%
where the time goes in v1:
time: 161 us; the launch traced here: 160 us
  Pallas kernels  129 us (80%)
  local copies, waits for them, and re-layouts  29.6 us (18%)
  other arithmetic  1.61 us (1%)
    pallas_call x1, Pallas kernels, gather(): pl.pallas_call(functools.partial(gather_kernel, n, width), out_shape=[jax...  129 us
    unnamed x7, local copies, waits for them, and re-layouts  28.3 us

profile of v1, /device:TPU:0, one launch (start us, length us, event | category | flops | bytes accessed | tf_op | source)
XLA Modules:
  0.0 160.4 jit_solution(6128095284481034230)
XLA Ops:
  0.6 0.7 add.5
  1.3 0.6 pad_bitcast_fusion.refs_12_
  1.9 128.5 %shard_map.173 = (bf16[4608,1024]{1,0:T(8,128)(2,1)}, bf16[4608,512]{1,0:T(8,128)(2,1)}, bf16[4608,512]{1,0:T(8,128)(2,1)}, bf16[4608,1024]{1,0:T(8,128)(2,1)}, f32[8,4,8,128]{3,2,1,0:T(8,128)}) custom-call(bf16[576,1024]{1,0:T(8,128)(2,1)} %refs_0_.1, bf16[576,512]{1,0:T(8,128)(2,1)} %refs_1_.1, bf16[576,512]{1,0:T(8,128)(2,1)} %refs_2_.1, ...), custom_call_target="tpu_custom_call" | custom-call | tf_op jit(solution)/shard_map/pallas_call | solution.py:186
  130.4 0.9 convert.4
  131.4 0.7 convert_element_type.6
  132.1 12.6 %copy.19 = bf16[1024,4608]{1,0:T(8,128)(2,1)} copy(bf16[1024,4608]{0,1:T(8,128)(2,1)} %bitcast.13) | data formatting | bytes 18874368
  144.7 8.5 %copy.26 = bf16[4608,1024]{1,0:T(8,128)(2,1)} copy(bf16[4608,1024]{1,0:T(8,128)(2,1)} %get-tuple-element.25) | data formatting | bytes 18874368
  153.2 0.0 copy-start
  153.2 5.0 %copy.27 = bf16[4608,512]{1,0:T(8,128)(2,1)} copy(bf16[4608,512]{1,0:T(8,128)(2,1)} %get-tuple-element.26) | data formatting | bytes 9437184
  158.2 0.0 copy-done
  158.2 2.2 %copy.28 = bf16[4608,512]{1,0:T(8,128)(2,1)} copy(bf16[4608,512]{1,0:T(8,128)(2,1)S(1)} %copy-done) | data formatting | bytes 9437184
  (2 shorter events, 0.0 us)
Async XLA Ops:
  153.2 5.0 %copy-start = (bf16[4608,512]{1,0:T(8,128)(2,1)S(1)}, bf16[4608,512]{1,0:T(8,128)(2,1)}, u32[]{:S(2)}) copy-start(bf16[4608,512]{1,0:T(8,128)(2,1)} %get-tuple-element.27) | copy-start | bytes 14155780

commit v2 on v1

--- a/solution.py
+++ b/solution.py
@@ -9,14 +9,17 @@
 from jax.sharding import PartitionSpec as P
 
 mix_rate = 0.5
+PIECES = 4
+GATHER_VMEM = 30 * 1024 * 1024
 MESH = pl.DeviceIdType.MESH
 
 
 def gather_kernel(n, width, *refs):
     trains, lows, highs, norm = refs[0:4], refs[4:8], refs[8:12], refs[12]
-    outs, norm_out = refs[13:17], refs[17]
-    mine, norm_row = refs[18:22], refs[22]
-    send_sem, recv_sem, norm_send, norm_recv, local_sem = refs[23:28]
+    turned_mixed, norm_out = refs[13], refs[17]
+    mine, mixed, norm_row = refs[18:22], refs[22], refs[23]
+    outs = (mixed,) + tuple(refs[14:17])
+    send_sem, recv_sem, norm_send, norm_recv, local_sem = refs[24:29]
 
     chips = n // 2
     side = math.isqrt(chips)
@@ -89,6 +92,33 @@
     streams = ([], [])
     aways = (after, before)
     partner_copies = []
+    mixed_copies = {}
+    pair = 2 * rows
+    per_chip = pair % 128 == 0
+
+    def forward(source, target, array, step):
+        copy = send(source, target, partner)
+        if array == 0 and per_chip:
+            mixed_copies.setdefault(step % chips, []).append(copy)
+        else:
+            partner_copies.append(copy)
+
+    def turn_columns(start, tiles):
+        def one(tile, carry):
+            place = pl.ds(pl.multiple_of(start + tile * 128, 128), 128)
+            turned_mixed[:, place] = mixed[place, :].T
+            return carry
+
+        lax.fori_loop(0, tiles, one, 0)
+
+    def turn_chip(step):
+        if per_chip:
+            for copy in mixed_copies.pop(step % chips):
+                copy.wait_recv()
+            if step == 0:
+                locals_[0].wait()
+            turn_columns((at(step) // 2) * pair, pair // 128)
+
     hops = chips // 2
 
     def send_own(direction, array, part):
@@ -130,7 +160,7 @@
         copy.start()
         locals_.append(copy)
         for part in range(2):
-            partner_copies.append(send(own(array, part), block(array, me, part), partner))
+            forward(own(array, part), block(array, me, part), array, 0)
 
     own_row.wait()
     for copy in row_copies:
@@ -150,6 +180,8 @@
         copy.start()
         table_copies.append(copy)
 
+    turn_chip(0)
+
     for hop in range(1, hops + 1):
         arriving = streams
         streams = ([], [])
@@ -163,7 +195,12 @@
                 if hop < hops and (not last or part == direction):
                     further = send(here, here, aways[direction])
                     streams[direction].append((further, array, part))
-                partner_copies.append(send(here, here, partner))
+                forward(here, here, array, hop if direction else -hop)
+            if hop == hops and turn == 1:
+                turn_chip(hop)
+        if hop < hops:
+            turn_chip(-hop)
+            turn_chip(hop)
 
     for copy in partner_copies:
         copy.wait_recv()
@@ -172,8 +209,10 @@
     for copy in table_copies:
         copy.wait()
     own_table.wait()
-    for copy in locals_:
+    for copy in locals_[1 if per_chip else 0 :]:
         copy.wait()
+    if not per_chip:
+        turn_columns(0, n * rows // 128)
 
 
 def gather(n, width, trains, lows, highs, norm):
@@ -185,15 +224,16 @@
     anywhere = pl.BlockSpec(memory_space=pl.ANY)
     return pl.pallas_call(
         functools.partial(gather_kernel, n, width),
-        out_shape=[
-            jax.ShapeDtypeStruct((n * train.shape[0], train.shape[1]), jnp.bfloat16)
-            for train in trains
+        out_shape=[pltpu.VMEM(trains[0].shape[1:] + (n * trains[0].shape[0],), jnp.bfloat16)]
+        + [
+            pltpu.VMEM((n * train.shape[0], train.shape[1]), jnp.bfloat16) for train in trains[1:]
         ]
         + [jax.ShapeDtypeStruct((n, width) + norm.shape, norm.dtype)],
         in_specs=[vmem] * 13,
-        out_specs=[anywhere] * 5,
+        out_specs=[vmem] * 4 + [anywhere],
         scratch_shapes=[pltpu.VMEM(train.shape, jnp.bfloat16) for train in trains]
         + [
+            pltpu.VMEM((n * trains[0].shape[0], trains[0].shape[1]), jnp.bfloat16),
             pltpu.VMEM((width,) + norm.shape, norm.dtype),
             pltpu.SemaphoreType.DMA((slots,)),
             pltpu.SemaphoreType.DMA((slots,)),
@@ -201,8 +241,39 @@
             pltpu.SemaphoreType.DMA((n + width - 2,)),
             pltpu.SemaphoreType.DMA((5,)),
         ],
-        compiler_params=pltpu.CompilerParams(collective_id=0, has_side_effects=True),
+        compiler_params=pltpu.CompilerParams(
+            collective_id=0, has_side_effects=True, vmem_limit_bytes=GATHER_VMEM
+        ),
     )(*trains, *lows, *highs, norm)
+
+
+def write_kernel(*refs):
+    arrays, sem = len(refs) // 2, refs[-1]
+    copies = []
+    for array in range(arrays):
+        source, target = refs[array], refs[arrays + array]
+        piece = source.shape[0] // PIECES
+        for cut in range(PIECES):
+            copy = pltpu.make_async_copy(
+                source.at[pl.ds(cut * piece, piece)],
+                target.at[pl.ds(cut * piece, piece)],
+                sem.at[array * PIECES + cut],
+            )
+            copy.start()
+            copies.append(copy)
+    for copy in copies:
+        copy.wait()
+
+
+def write_out(arrays):
+    return pl.pallas_call(
+        write_kernel,
+        out_shape=[jax.ShapeDtypeStruct(array.shape, array.dtype) for array in arrays],
+        in_specs=[pl.BlockSpec(memory_space=pltpu.VMEM)] * len(arrays),
+        out_specs=[pl.BlockSpec(memory_space=pltpu.HBM)] * len(arrays),
+        scratch_shapes=[pltpu.SemaphoreType.DMA((len(arrays) * PIECES,))],
+        compiler_params=pltpu.CompilerParams(vmem_limit_bytes=1024 * 1024),
+    )(*arrays)
 
 
 def on_device(
@@ -226,16 +297,17 @@
     share = norm_train.shape[0]
     lanes = -(-share // 1024) * 1024
     norm = jnp.pad(norm_train + norm_step, (0, lanes - share)).reshape(-1, 128)
-    query, key, value, mixed, table = gather(
+    *gathered, table = gather(
         n,
         width,
-        (train_query, train_key, train_value, train_mixed.T),
-        (low_query.T, low_key.T, low_value.T, high_mixed),
-        (high_query, high_key, high_value, low_mixed.T),
+        (train_mixed.T, train_query, train_key, train_value),
+        (high_mixed, low_query.T, low_key.T, low_value.T),
+        (low_mixed.T, high_query, high_key, high_value),
         norm,
     )
+    mixed, query, key, value = write_out(gathered)
     serve_norm = table.reshape(n * width, -1)[:, :share].reshape(-1).astype(jnp.bfloat16)
-    return (query, key, value, mixed.T, serve_norm)
+    return (query, key, value, mixed, serve_norm)
 
 
 def solution(mesh):

time: 161 us -> 140 us (0.87)
  local copies, waits for them, and re-layouts: 29.6 us -> 1.32 us
  Pallas kernels: 129 us -> 137 us
    unnamed x7 -> x3, local copies, waits for them, and re-layouts: 28.3 us -> 0.02 us
    pallas_call x1 -> x2, Pallas kernels: 129 us -> 137 us  [the longest x1 127 us: gather(): pl.pallas_call(functools.partial(gather_kernel, n, width), out_shape=[plt...]
where the time goes in v2:
time: 140 us; the launch traced here: 139 us
  Pallas kernels  137 us (98%)
    pallas_call x1, Pallas kernels, gather(): pl.pallas_call(functools.partial(gather_kernel, n, width), out_shape=[plt...  127 us
    pallas_call x1, Pallas kernels, write_out(): pl.pallas_call(write_kernel, out_shape=[jax.ShapeDtypeStruct(array.shape,...  9.45 us

profile of v2, /device:TPU:0, one launch (start us, length us, event | category | flops | bytes accessed | tf_op | source)
XLA Modules:
  0.0 139.4 jit_solution(15682042975372298849)
XLA Ops:
  0.6 0.7 add.5
  1.3 0.6 pad_bitcast_fusion.refs_12_
  1.9 127.2 %shard_map.173 = (bf16[1024,4608]{1,0:T(8,128)(2,1)S(1)}, bf16[4608,1024]{1,0:T(8,128)(2,1)S(1)}, bf16[4608,512]{1,0:T(8,128)(2,1)S(1)}, bf16[4608,512]{1,0:T(8,128)(2,1)S(1)}, f32[8,4,8,128]{3,2,1,0:T(8,128)}) custom-call(bf16[576,1024]{1,0:T(8,128)(2,1)} %bitcast.12, bf16[576,1024]{1,0:T(8,128)(2,1)} %refs_1_.1, bf16[576,512]{1,0:T(8,128)(2,1)} %refs_2_.1, ...), custom_call_target="tpu_custom_call" | custom-call | tf_op jit(solution)/shard_map/pallas_call | solution.py:225
  129.2 0.0 copy-start
  129.2 9.5 %shard_map.174 = (bf16[1024,4608]{1,0:T(8,128)(2,1)}, bf16[4608,1024]{1,0:T(8,128)(2,1)}, bf16[4608,512]{1,0:T(8,128)(2,1)}, bf16[4608,512]{1,0:T(8,128)(2,1)}) custom-call(bf16[1024,4608]{1,0:T(8,128)(2,1)S(1)} %get-tuple-element.14.refs_0_, bf16[4608,1024]{1,0:T(8,128)(2,1)S(1)} %get-tuple-element.15.refs_1_, ...), custom_call_target="tpu_custom_call" | custom-call | tf_op jit(solution)/shard_map/pallas_call | solution.py:269
  138.6 0.0 copy-done
  138.7 0.7 convert_element_type.6
  (3 shorter events, 0.0 us)
Async XLA Ops:
  129.2 9.5 %copy-start = (f32[8,4,8,128]{3,2,1,0:T(8,128)S(1)}, f32[8,4,8,128]{3,2,1,0:T(8,128)}, u32[]{:S(2)}) copy-start(f32[8,4,8,128]{3,2,1,0:T(8,128)} %get-tuple-element.22) | copy-start | bytes 393220

commit v3 on v2

--- a/solution.py
+++ b/solution.py
@@ -43,6 +43,12 @@
 
     after, before = at(1), at(-1)
     partner = chip * 2 + (1 - core)
+
+    loads = []
+    for array in range(4):
+        copy = pltpu.make_async_copy(trains[array], mine[array], local_sem.at[array])
+        copy.start()
+        loads.append(copy)
 
     barrier = pltpu.get_barrier_semaphore()
     for step in range(1, n):
@@ -86,7 +92,8 @@
             (((0,), (0,)), ((), ())),
             preferred_element_type=jnp.float32,
         )
-        merged = trains[array][...].astype(jnp.float32) + mix_rate * delta
+        loads[array].wait()
+        merged = mine[array][...].astype(jnp.float32) + mix_rate * delta
         mine[array][...] = merged.astype(jnp.bfloat16)
 
     streams = ([], [])
@@ -229,7 +236,7 @@
             pltpu.VMEM((n * train.shape[0], train.shape[1]), jnp.bfloat16) for train in trains[1:]
         ]
         + [jax.ShapeDtypeStruct((n, width) + norm.shape, norm.dtype)],
-        in_specs=[vmem] * 13,
+        in_specs=[anywhere] * 4 + [vmem] * 9,
         out_specs=[vmem] * 4 + [anywhere],
         scratch_shapes=[pltpu.VMEM(train.shape, jnp.bfloat16) for train in trains]
         + [
@@ -294,9 +301,7 @@
     norm_train,
     norm_step,
 ):
-    share = norm_train.shape[0]
-    lanes = -(-share // 1024) * 1024
-    norm = jnp.pad(norm_train + norm_step, (0, lanes - share)).reshape(-1, 128)
+    norm = (norm_train + norm_step).reshape(1, -1)
     *gathered, table = gather(
         n,
         width,
@@ -306,7 +311,7 @@
         norm,
     )
     mixed, query, key, value = write_out(gathered)
-    serve_norm = table.reshape(n * width, -1)[:, :share].reshape(-1).astype(jnp.bfloat16)
+    serve_norm = table.reshape(-1).astype(jnp.bfloat16)
     return (query, key, value, mixed, serve_norm)
 
 

time: 140 us -> 138 us (0.986)
  Pallas kernels: 137 us -> 135 us
    pallas_call x1, Pallas kernels: 127 us -> 125 us  [gather(): pl.pallas_call(functools.partial(gather_kernel, n, width), out_shape=[plt...]
where the time goes in v3:
time: 138 us; the launch traced here: 137 us
  Pallas kernels  135 us (98%)
    pallas_call x1, Pallas kernels, gather(): pl.pallas_call(functools.partial(gather_kernel, n, width), out_shape=[plt...  125 us
    pallas_call x1, Pallas kernels, write_out(): pl.pallas_call(write_kernel, out_shape=[jax.ShapeDtypeStruct(array.shape,...  9.45 us

profile of v3, /device:TPU:0, one launch (start us, length us, event | category | flops | bytes accessed | tf_op | source)
XLA Modules:
  0.0 137.3 jit_solution(8878939262759455991)
XLA Ops:
  0.6 1.3 add.3
  1.9 125.2 %shard_map.173 = (bf16[1024,4608]{1,0:T(8,128)(2,1)S(1)}, bf16[4608,1024]{1,0:T(8,128)(2,1)S(1)}, bf16[4608,512]{1,0:T(8,128)(2,1)S(1)}, bf16[4608,512]{1,0:T(8,128)(2,1)S(1)}, f32[8,4,1,144]{3,2,1,0:T(1,128)}) custom-call(bf16[576,1024]{1,0:T(8,128)(2,1)} %bitcast.6, bf16[576,1024]{1,0:T(8,128)(2,1)} %refs_1_.1, bf16[576,512]{1,0:T(8,128)(2,1)} %refs_2_.1, ...), custom_call_target="tpu_custom_call" | custom-call | tf_op jit(solution)/shard_map/pallas_call | solution.py:232
  127.1 0.0 copy-start
  127.1 9.5 %shard_map.174 = (bf16[1024,4608]{1,0:T(8,128)(2,1)}, bf16[4608,1024]{1,0:T(8,128)(2,1)}, bf16[4608,512]{1,0:T(8,128)(2,1)}, bf16[4608,512]{1,0:T(8,128)(2,1)}) custom-call(bf16[1024,4608]{1,0:T(8,128)(2,1)S(1)} %get-tuple-element.14.refs_0_, bf16[4608,1024]{1,0:T(8,128)(2,1)S(1)} %get-tuple-element.15.refs_1_, ...), custom_call_target="tpu_custom_call" | custom-call | tf_op jit(solution)/shard_map/pallas_call | solution.py:276
  136.5 0.0 copy-done
  136.5 0.1 convert_reduce_fusion
  136.6 0.7 convert_element_type.7
Async XLA Ops:
  127.1 9.5 %copy-start = (f32[8,4,1,144]{3,2,1,0:T(1,128)S(1)}, f32[8,4,1,144]{3,2,1,0:T(1,128)}, u32[]{:S(2)}) copy-start(f32[8,4,1,144]{3,2,1,0:T(1,128)} %get-tuple-element.22) | copy-start | bytes 55300
